TPU v7x, 512 devices: a 4x2x32 block of a 4x16x32 slice. The times are simulated.
512 devices in a mesh: groups: 2 (over y), row: 32 (over z), col: 4 (over x), sub: 2 (over core).
Axes of the slice: x: 4, y: 2, z: 32, core: 2. Of those that a mesh axis runs over, the one named last changes fastest.
The devices are a block of a 4x16x32 slice.
Arguments:
- matrix: float32 [16384, 8192], P(('groups', 'row'), ('col', 'sub')), parts along dimension 0, may hold values from -60 to 60
- basis_vectors: float32 [16384, 1024], P(('groups', 'row'), ('col', 'sub')), parts along dimension 0, may hold values from -0.0625 to 0.0625
- split_size: int32 [2], P('groups'), parts along dimension 0, may hold values from 256 to 767
Outputs:
- children: float32 [2, 2048, 1024], P('sub', ('groups', 'row'), 'col'), parts along dimension 1
There are 2 independent parts, one for each index of `groups`. A program takes and returns all parts, laid end to end along the dimension named above; each array names one. Nothing has to cross between parts.
Inputs may be any that keep to these rules, and one draw needn't show every extreme that they name: The second subspace has 1024 minus split_size vectors.
All inputs are finite; a program needn't handle non-finite values.
Results may differ from a plain program's by a relative error of at most 0.00011.
Values sent between devices are 32-bit elements; how exact they have to be, the bound alone decides.
No kernel may reach another device: no remote copies, remote signals or barrier semaphores. Data moves between devices by JAX's collectives and lax.ppermute only.
A program may use at most 64 MiB of HBM per device.

v0:
```python
import jax
import jax.numpy as jnp
from jax import lax
from jax.sharding import PartitionSpec as P

PRECISION = lax.Precision.HIGHEST
NEAR = 4


def shifted(array, axis, step):
    size = lax.axis_size(axis)
    return lax.ppermute(array, axis, [(i, (i + step) % size) for i in range(size)])


def swapped(array, axis):
    size = lax.axis_size(axis)
    return lax.ppermute(array, axis, [(i, i ^ 1) for i in range(size)])


def product(left, right, contract):
    return lax.dot_general(
        left, right, (contract, ((), ())), precision=PRECISION, preferred_element_type=jnp.float32
    )


def all_columns(basis):
    half = basis.shape[0] // 2
    parts = [
        lax.all_gather(basis[i * half : (i + 1) * half], ("col", "sub"), axis=0) for i in range(2)
    ]
    return parts


def shards(matrix, basis_vectors, split_size):
    rows_here, width = matrix.shape
    n_row = lax.axis_size("row")
    n_col = lax.axis_size("col")
    row = lax.axis_index("row")
    col = lax.axis_index("col")
    sub = lax.axis_index("sub")
    parity = row % 2
    every_other = [[first + 2 * i for i in range(n_row // 2)] for first in range(2)]
    strip = lax.all_gather(basis_vectors, "row", axis=0, tiled=True, axis_index_groups=every_other)
    blocks = matrix.reshape(rows_here, width // (2 * rows_here), 2, rows_here)
    keep = jnp.where(parity == 0, blocks[:, :, 0], blocks[:, :, 1]).reshape(rows_here, width // 2)
    give = jnp.where(parity == 0, blocks[:, :, 1], blocks[:, :, 0]).reshape(rows_here, width // 2)
    own = jnp.concatenate([keep, swapped(give, "row")], axis=0)
    before = shifted(own, "col", 1)
    after = shifted(own, "col", -1)
    half = own.shape[0] // 2
    across = jnp.concatenate(
        [shifted(before[:half], "col", 1), shifted(after[half:], "col", -1)], axis=0
    )
    pieces = {0: own, 1: before, 2: across, 3: after}
    mate = swapped(basis_vectors, "row")
    pair_basis = jnp.concatenate(all_columns(basis_vectors) + all_columns(mate), axis=1)
    span = own.shape[1]
    image = None
    for distance, piece in pieces.items():
        source = (col - distance) % n_col
        other = swapped(piece, "sub")
        for core, operand in ((sub, piece), (1 - sub, other)):
            rows = lax.dynamic_slice_in_dim(strip, (source * 2 + core) * span, span, 0)
            part = product(operand, rows, ((1,), (0,)))
            image = part if image is None else image + part
    partial = product(pair_basis, image, ((1,), (0,)))
    total = partial.shape[0] * partial.shape[1]
    share = total // n_row
    far = n_row // NEAR
    partial = partial.reshape(far, NEAR, share, -1).swapaxes(0, 1)
    near_groups = [[NEAR * g + q for q in range(NEAR)] for g in range(far)]
    far_groups = [[NEAR * g + q for g in range(far)] for q in range(NEAR)]
    partial = lax.all_to_all(partial, "row", 0, 0, tiled=True, axis_index_groups=near_groups).sum(0)
    proj_block = lax.all_to_all(partial, "row", 0, 0, tiled=True, axis_index_groups=far_groups).sum(
        0
    )
    child_block = lax.all_gather(proj_block, "sub", axis=1, tiled=True)
    row_ids = jnp.arange(child_block.shape[0], dtype=jnp.int32) + row * child_block.shape[0]
    col_ids = jnp.arange(child_block.shape[1], dtype=jnp.int32) + col * child_block.shape[1]
    leading = split_size[0]
    row_first = row_ids < leading
    col_first = col_ids < leading
    mask_one = row_first[:, None] & col_first[None, :]
    mask_two = jnp.logical_not(row_first)[:, None] & jnp.logical_not(col_first)[None, :]
    selected = jnp.where(sub == 0, mask_one, mask_two)
    return jnp.where(selected, child_block, jnp.zeros((), jnp.float32))[None]


def solution(mesh):
    placed = (
        P(("groups", "row"), ("col", "sub")),
        P(("groups", "row"), ("col", "sub")),
        P("groups"),
    )
    return jax.shard_map(
        shards,
        mesh=mesh,
        in_specs=placed,
        out_specs=P("sub", ("groups", "row"), "col"),
        check_vma=False,
    )
```

profile of v0, /device:TPU:41, one launch (start us, length us, event | category | flops | bytes accessed | tf_op | source)
XLA Modules:
  0.0 284.6 jit_solution(17117127371487717278)
XLA Ops:
  7.3 2.1 reshape.32
  9.4 3.5 %fusion.14 = (f32[256,2,256]{2,1,0:T(2,128)S(1)}, f32[256,2,256]{2,1,0:T(2,128)S(1)}) fusion(pred[]{:T(512)S(6)} %eq.14, f32[256,2,2,256]{3,2,1,0:T(2,128)S(1)} %reshape.32), kind=kLoop, calls=%fused_computation.19 | loop fusion | flops 262144 | bytes 2097153 | tf_op jit(solution)/shard_map/jit(_where)/select_n | solution.py:46
  13.0 4.4 %collective-permute-start.1 = (f32[256,512]{1,0:T(8,128)S(1)}, f32[256,512]{1,0:T(8,128)S(1)}, u32[]{:S(2)}, u32[]{:S(2)}) collective-permute-start(f32[256,512]{1,0:T(8,128)S(1)} %bitcast.36), channel_id=1, source_target_pairs={{0,8},{8,0},{16,24},{24,16},{32,40},{40,32},{48,56},{56,48},{64,72... | collective-permute-start | bytes 1572872 | tf_op jit(solution)/shard_map/ppermute | solution.py:17
  17.5 11.6 %collective-permute-done.1 = f32[256,512]{1,0:T(8,128)S(1)} collective-permute-done((f32[256,512]{1,0:T(8,128)S(1)}, f32[256,512]{1,0:T(8,128)S(1)}, u32[]{:S(2)}, u32[]{:S(2)}) %collective-permute-start.1) | collective-permute-done | bytes 524320 | tf_op jit(solution)/shard_map/ppermute | solution.py:17
  29.2 3.3 %collective-permute-start.3 = (f32[512,512]{1,0:T(8,128)S(1)}, f32[512,512]{1,0:T(8,128)S(1)}, u32[]{:S(2)}, u32[]{:S(2)}) collective-permute-start(f32[512,512]{1,0:T(8,128)S(1)} %constant_dynamic-update-slice_fusion), channel_id=1, source_target_pairs={{0,2},{2,4},{4,6},{6,0},{1,3},{3,5},{5,7},{7,1},{8,10},{10,12},{12... | collective-permute-start | bytes 3145736 | tf_op jit(solution)/shard_map/ppermute | solution.py:12
  32.5 3.5 %collective-permute-start.6 = (f32[512,512]{1,0:T(8,128)S(1)}, f32[512,512]{1,0:T(8,128)S(1)}, u32[]{:S(2)}, u32[]{:S(2)}) collective-permute-start(f32[512,512]{1,0:T(8,128)S(1)} %constant_dynamic-update-slice_fusion), channel_id=1, source_target_pairs={{0,6},{2,0},{4,2},{6,4},{1,7},{3,1},{5,3},{7,5},{8,14},{10,8},{12,... | collective-permute-start | bytes 3145736 | tf_op jit(solution)/shard_map/ppermute | solution.py:12
  36.0 3.1 %collective-permute-start = (f32[256,128]{1,0:T(8,128)S(1)}, f32[256,128]{1,0:T(8,128)S(1)}, u32[]{:S(2)}, u32[]{:S(2)}) collective-permute-start(f32[256,128]{1,0:T(8,128)S(1)} %copy-done.5), channel_id=1, source_target_pairs={{0,8},{8,0},{16,24},{24,16},{32,40},{40,32},{48,56},{56,48},{64,72... | collective-permute-start | bytes 393224 | tf_op jit(solution)/shard_map/ppermute | solution.py:17
  39.1 30.1 %all-gather = f32[1024,128]{1,0:T(8,128)} all-gather(f32[128,128]{1,0:T(8,128)S(1)} %get-tuple-element.11), channel_id=2, replica_groups=mesh['groups'=2,'row'=32,'col'=4,'sub'=2] {'col','sub'}, dimensions={0}, use_global_device_ids=true | all-gather | bytes 589824 | tf_op jit(solution)/shard_map/all_gather | solution.py:29
  70.1 3.5 %collective-permute-start.5 = (f32[256,512]{1,0:T(8,128)}, f32[256,512]{1,0:T(8,128)}, u32[]{:S(2)}, u32[]{:S(2)}) collective-permute-start(f32[256,512]{1,0:T(8,128)} %slice.38), channel_id=1, source_target_pairs={{0,2},{2,4},{4,6},{6,0},{1,3},{3,5},{5,7},{7,1},{8,10},{10,12},{12... | collective-permute-start | bytes 1572872 | tf_op jit(solution)/shard_map/ppermute | solution.py:12
  73.6 23.2 %all-gather.1 = f32[1024,128]{1,0:T(8,128)} all-gather(f32[128,128]{1,0:T(8,128)S(1)} %get-tuple-element.12), channel_id=3, replica_groups=mesh['groups'=2,'row'=32,'col'=4,'sub'=2] {'col','sub'}, dimensions={0}, use_global_device_ids=true | all-gather | bytes 589824 | tf_op jit(solution)/shard_map/all_gather | solution.py:29
  96.8 2.0 copy.13
  98.9 2.1 copy.14
  101.0 3.4 %collective-permute-start.7 = (f32[256,512]{1,0:T(8,128)S(1)}, f32[256,512]{1,0:T(8,128)S(1)}, u32[]{:S(2)}, u32[]{:S(2)}) collective-permute-start(f32[256,512]{1,0:T(8,128)S(1)} %slice.39), channel_id=1, source_target_pairs={{0,6},{2,0},{4,2},{6,4},{1,7},{3,1},{5,3},{7,5},{8,14},{10,8},{12,... | collective-permute-start | bytes 1572872 | tf_op jit(solution)/shard_map/ppermute | solution.py:12
  104.4 21.8 %all-gather.2 = f32[1024,128]{1,0:T(8,128)} all-gather(f32[128,128]{1,0:T(8,128)S(1)} %get-tuple-element.13), channel_id=4, replica_groups=mesh['groups'=2,'row'=32,'col'=4,'sub'=2] {'col','sub'}, dimensions={0}, use_global_device_ids=true | all-gather | bytes 589824 | tf_op jit(solution)/shard_map/all_gather | solution.py:29
  126.2 2.1 collective-permute-start.2
  128.3 1.9 constant_dynamic-update-slice_fusion.3
  131.0 2.3 collective-permute-start.8
  133.3 14.5 %all-gather.3 = f32[1024,128]{1,0:T(8,128)} all-gather(f32[128,128]{1,0:T(8,128)S(1)} %get-tuple-element.14), channel_id=5, replica_groups=mesh['groups'=2,'row'=32,'col'=4,'sub'=2] {'col','sub'}, dimensions={0}, use_global_device_ids=true | all-gather | bytes 589824 | tf_op jit(solution)/shard_map/all_gather | solution.py:29
  147.8 2.1 copy.15
  149.9 2.1 copy.16
  152.0 2.1 collective-permute-start.4
  154.1 2.3 collective-permute-start.9
  156.4 2.1 fusion.23
  158.5 2.3 fusion.20
  161.8 2.2 fusion.25
  164.0 2.2 fusion.18
  167.3 2.4 fusion.11
  169.7 2.2 fusion.8
  173.8 20.8 %all_to_all.10 = f32[4,8,32,128]{3,2,1,0:T(8,128)S(1)} all-to-all(f32[4,8,32,128]{3,2,1,0:T(8,128)S(1)} %bitcast.35), channel_id=1, replica_groups={{0,8,16,24},{32,40,48,56},{64,72,80,88},{96,104,112,120},{128,136,144,1..., dimensions={0} | all-to-all | bytes 1048576 | tf_op jit(solution)/shard_map/all_to_all | solution.py:73
  195.3 49.8 %all-to-all-start.1 = ((f32[8,32,128]{2,1,0:T(8,128)}), f32[8,32,128]{2,1,0:T(8,128)S(1)}, u32[]{:S(2)}, u32[]{:S(2)}) async-start(f32[8,32,128]{2,1,0:T(8,128)} %reduce_sum.18), calls=%async_computation.1 | async-start | bytes 262144 | tf_op jit(solution)/shard_map/all_to_all | solution.py:74
  245.8 23.3 %all-to-all-done.1 = f32[8,32,128]{2,1,0:T(8,128)S(1)} async-done(((f32[8,32,128]{2,1,0:T(8,128)}), f32[8,32,128]{2,1,0:T(8,128)S(1)}, u32[]{:S(2)}, u32[]{:S(2)}) %all-to-all-start.1) | async-done | bytes 131104 | tf_op jit(solution)/shard_map/all_to_all | solution.py:74
  269.1 8.0 %all_gather.39 = f32[32,256]{1,0:T(8,128)S(1)} all-gather(f32[32,128]{1,0:T(8,128)S(1)} %reduce_sum.19), channel_id=1, replica_groups=mesh['groups'=2,'row'=32,'col'=4,'sub'=2] {'sub'}, dimensions={1}, use_global_device_ids=true | all-gather | bytes 49152 | tf_op jit(solution)/shard_map/all_gather | solution.py:77
  (42 shorter events, 7.9 us)
Async XLA Ops:
  6.5 149.8 %all-gather.6.cloned.1.call-start = ((), (), s32[]{:S(2)}) async-start(), calls=%async_computation.2 | async-start | bytes 2228224 | tf_op jit(solution)/shard_map/all_gather | solution.py:43
  13.0 23.0 %copy-start.5 = (f32[256,128]{1,0:T(8,128)S(1)}, f32[256,128]{1,0:T(8,128)}, u32[]{:S(2)}) copy-start(f32[256,128]{1,0:T(8,128)} %param.4) | copy-start | bytes 393220
  13.0 16.1 %collective-permute-start.1 = (f32[256,512]{1,0:T(8,128)S(1)}, f32[256,512]{1,0:T(8,128)S(1)}, u32[]{:S(2)}, u32[]{:S(2)}) collective-permute-start(f32[256,512]{1,0:T(8,128)S(1)} %bitcast.36), channel_id=1, source_target_pairs={{0,8},{8,0},{16,24},{24,16},{32,40},{40,32},{48,56},{56,48},{64,72... | collective-permute-start | bytes 1572872 | tf_op jit(solution)/shard_map/ppermute | solution.py:17
  29.2 40.1 %collective-permute-start.3 = (f32[512,512]{1,0:T(8,128)S(1)}, f32[512,512]{1,0:T(8,128)S(1)}, u32[]{:S(2)}, u32[]{:S(2)}) collective-permute-start(f32[512,512]{1,0:T(8,128)S(1)} %constant_dynamic-update-slice_fusion), channel_id=1, source_target_pairs={{0,2},{2,4},{4,6},{6,0},{1,3},{3,5},{5,7},{7,1},{8,10},{10,12},{12... | collective-permute-start | bytes 3145736 | tf_op jit(solution)/shard_map/ppermute | solution.py:12
  32.5 68.5 %collective-permute-start.6 = (f32[512,512]{1,0:T(8,128)S(1)}, f32[512,512]{1,0:T(8,128)S(1)}, u32[]{:S(2)}, u32[]{:S(2)}) collective-permute-start(f32[512,512]{1,0:T(8,128)S(1)} %constant_dynamic-update-slice_fusion), channel_id=1, source_target_pairs={{0,6},{2,0},{4,2},{6,4},{1,7},{3,1},{5,3},{7,5},{8,14},{10,8},{12,... | collective-permute-start | bytes 3145736 | tf_op jit(solution)/shard_map/ppermute | solution.py:12
  36.0 68.4 %collective-permute-start = (f32[256,128]{1,0:T(8,128)S(1)}, f32[256,128]{1,0:T(8,128)S(1)}, u32[]{:S(2)}, u32[]{:S(2)}) collective-permute-start(f32[256,128]{1,0:T(8,128)S(1)} %copy-done.5), channel_id=1, source_target_pairs={{0,8},{8,0},{16,24},{24,16},{32,40},{40,32},{48,56},{56,48},{64,72... | collective-permute-start | bytes 393224 | tf_op jit(solution)/shard_map/ppermute | solution.py:17
  70.1 58.2 %collective-permute-start.5 = (f32[256,512]{1,0:T(8,128)}, f32[256,512]{1,0:T(8,128)}, u32[]{:S(2)}, u32[]{:S(2)}) collective-permute-start(f32[256,512]{1,0:T(8,128)} %slice.38), channel_id=1, source_target_pairs={{0,2},{2,4},{4,6},{6,0},{1,3},{3,5},{5,7},{7,1},{8,10},{10,12},{12... | collective-permute-start | bytes 1572872 | tf_op jit(solution)/shard_map/ppermute | solution.py:12
  101.0 29.2 %collective-permute-start.7 = (f32[256,512]{1,0:T(8,128)S(1)}, f32[256,512]{1,0:T(8,128)S(1)}, u32[]{:S(2)}, u32[]{:S(2)}) collective-permute-start(f32[256,512]{1,0:T(8,128)S(1)} %slice.39), channel_id=1, source_target_pairs={{0,6},{2,0},{4,2},{6,4},{1,7},{3,1},{5,3},{7,5},{8,14},{10,8},{12,... | collective-permute-start | bytes 1572872 | tf_op jit(solution)/shard_map/ppermute | solution.py:12
  126.2 35.6 %collective-permute-start.2 = (f32[512,512]{1,0:T(8,128)S(1)}, f32[512,512]{1,0:T(8,128)}, u32[]{:S(2)}, u32[]{:S(2)}) collective-permute-start(f32[512,512]{1,0:T(8,128)S(1)} %constant_dynamic-update-slice_fusion), channel_id=1, source_target_pairs={{0,1},{1,0},{2,3},{3,2},{4,5},{5,4},{6,7},{7,6},{8,9},{9,8},{10,11... | collective-permute-start | bytes 3145736 | tf_op jit(solution)/shard_map/ppermute | solution.py:17
  131.0 33.0 %collective-permute-start.8 = (f32[512,512]{1,0:T(8,128)}, f32[512,512]{1,0:T(8,128)}, u32[]{:S(2)}, u32[]{:S(2)}) collective-permute-start(f32[512,512]{1,0:T(8,128)} %constant_dynamic-update-slice_fusion.2), channel_id=1, source_target_pairs={{0,1},{1,0},{2,3},{3,2},{4,5},{5,4},{6,7},{7,6},{8,9},{9,8},{10,11... | collective-permute-start | bytes 3145736 | tf_op jit(solution)/shard_map/ppermute | solution.py:17
  152.0 15.3 %collective-permute-start.4 = (f32[512,512]{1,0:T(8,128)S(1)}, f32[512,512]{1,0:T(8,128)}, u32[]{:S(2)}, u32[]{:S(2)}) collective-permute-start(f32[512,512]{1,0:T(8,128)S(1)} %collective-permute-done.3), channel_id=1, source_target_pairs={{0,1},{1,0},{2,3},{3,2},{4,5},{5,4},{6,7},{7,6},{8,9},{9,8},{10,11... | collective-permute-start | bytes 3145736 | tf_op jit(solution)/shard_map/ppermute | solution.py:17
  154.1 15.6 %collective-permute-start.9 = (f32[512,512]{1,0:T(8,128)S(1)}, f32[512,512]{1,0:T(8,128)}, u32[]{:S(2)}, u32[]{:S(2)}) collective-permute-start(f32[512,512]{1,0:T(8,128)S(1)} %collective-permute-done.6), channel_id=1, source_target_pairs={{0,1},{1,0},{2,3},{3,2},{4,5},{5,4},{6,7},{7,6},{8,9},{9,8},{10,11... | collective-permute-start | bytes 3145736 | tf_op jit(solution)/shard_map/ppermute | solution.py:17
  156.4 4.4 %copy-start = (f32[4096,128]{1,0:T(8,128)S(1)}, f32[4096,128]{1,0:T(8,128)}, u32[]{:S(2)}) copy-start(f32[4096,128]{1,0:T(8,128)} %all-gather.6.cloned.1.call-done) | copy-start | bytes 6291460
  167.2 4.7 %copy-start.1 = (f32[8,128,128]{1,2,0:T(8,128)S(1)}, f32[8,128,128]{1,2,0:T(8,128)}, u32[]{:S(2)}) copy-start(f32[8,128,128]{1,2,0:T(8,128)} %copy.13) | copy-start | bytes 1572868
  167.2 4.7 %copy-start.2 = (f32[8,128,128]{1,2,0:T(8,128)S(1)}, f32[8,128,128]{1,2,0:T(8,128)}, u32[]{:S(2)}) copy-start(f32[8,128,128]{1,2,0:T(8,128)} %copy.14) | copy-start | bytes 1572868
  167.3 4.7 %copy-start.3 = (f32[8,128,128]{1,2,0:T(8,128)S(1)}, f32[8,128,128]{1,2,0:T(8,128)}, u32[]{:S(2)}) copy-start(f32[8,128,128]{1,2,0:T(8,128)} %copy.15) | copy-start | bytes 1572868
  167.3 4.7 %copy-start.4 = (f32[8,128,128]{1,2,0:T(8,128)S(1)}, f32[8,128,128]{1,2,0:T(8,128)}, u32[]{:S(2)}) copy-start(f32[8,128,128]{1,2,0:T(8,128)} %copy.16) | copy-start | bytes 1572868
  195.3 73.8 %all-to-all-start.1 = ((f32[8,32,128]{2,1,0:T(8,128)}), f32[8,32,128]{2,1,0:T(8,128)S(1)}, u32[]{:S(2)}, u32[]{:S(2)}) async-start(f32[8,32,128]{2,1,0:T(8,128)} %reduce_sum.18), calls=%async_computation.1 | async-start | bytes 262144 | tf_op jit(solution)/shard_map/all_to_all | solution.py:74
Sparse Core Ops, SparseCore 0:
  9.4 122.9 all-gather.5
where the time goes:
time: 286 us; the launch traced here: 285 us
  blocking collectives  119 us (42%)
  starting transfers between devices  79.8 us (28%)
  waiting for transfers between devices  35.7 us (12%)
  matrix products  17.1 us (6%)
  between operations  14.5 us (5%)
  local copies, waits for them, and re-layouts  14.2 us (5%)
  other arithmetic  4.92 us (2%)
    all_gather x4, blocking collectives, all_columns(): lax.all_gather(basis[i * half:(i + 1) * half], ('col', 'sub'), axis=0)  89.7 us
    all_to_all x1, starting transfers between devices, shards(): lax.all_to_all(partial, 'row', 0, 0, tiled=True, axis_index_groups=far_gr...  49.8 us
    all_to_all x1, waiting for transfers between devices, shards(): lax.all_to_all(partial, 'row', 0, 0, tiled=True, axis_index_groups=far_gr...  23.3 us
    all_to_all x1, blocking collectives, shards(): lax.all_to_all(partial, 'row', 0, 0, tiled=True, axis_index_groups=near_g...  20.8 us
    dot_general x9, matrix products, product(): lax.dot_general(left, right, (contract, ((), ())), precision=PRECISION, p...  17.1 us
    ppermute x6, starting transfers between devices, swapped(): return lax.ppermute(array, axis, [(i, i ^ 1) for i in range(size)])  16.3 us
    ppermute x4, starting transfers between devices, shifted(): lax.ppermute(array, axis, [(i, (i + step) % size) for i in range(size)])  13.7 us
    ppermute x6, waiting for transfers between devices, swapped(): return lax.ppermute(array, axis, [(i, i ^ 1) for i in range(size)])  11.6 us
  transfers between devices with their start and end apart: 12, of which 2 were waited for; matrix products, arithmetic and copies ran while one was open for 11% of the time, Pallas kernels for 0%

commit v1 on v0

--- a/solution.py
+++ b/solution.py
@@ -74,7 +74,9 @@
     proj_block = lax.all_to_all(partial, "row", 0, 0, tiled=True, axis_index_groups=far_groups).sum(
         0
     )
-    child_block = lax.all_gather(proj_block, "sub", axis=1, tiled=True)
+    child_block = jnp.concatenate(
+        lax.all_to_all(jnp.stack([proj_block] * lax.axis_size("sub")), "sub", 0, 0), axis=1
+    )
     row_ids = jnp.arange(child_block.shape[0], dtype=jnp.int32) + row * child_block.shape[0]
     col_ids = jnp.arange(child_block.shape[1], dtype=jnp.int32) + col * child_block.shape[1]
     leading = split_size[0]

time: 286 us -> 288 us (level)
    all_to_all x0 -> x1, blocking collectives: none -> 9.88 us  [shards(): lax.all_to_all(jnp.stack([proj_block] * lax.axis_size('sub')), 'sub', 0, 0)]
    all_gather x1 -> x0, blocking collectives: 7.99 us -> none  [shards(): child_block = lax.all_gather(proj_block, 'sub', axis=1, tiled=True)]
where the time goes in v1:
time: 288 us; the launch traced here: 287 us
  blocking collectives  120 us (42%)
  starting transfers between devices  79.8 us (28%)
  waiting for transfers between devices  35.7 us (12%)
  matrix products  17.1 us (6%)
  between operations  14.5 us (5%)
  local copies, waits for them, and re-layouts  14.2 us (5%)
  other arithmetic  4.93 us (2%)
    all_gather x4, blocking collectives, all_columns(): lax.all_gather(basis[i * half:(i + 1) * half], ('col', 'sub'), axis=0)  89.7 us
    all_to_all x1, starting transfers between devices, shards(): lax.all_to_all(partial, 'row', 0, 0, tiled=True, axis_index_groups=far_gr...  49.8 us
    all_to_all x1, waiting for transfers between devices, shards(): lax.all_to_all(partial, 'row', 0, 0, tiled=True, axis_index_groups=far_gr...  23.3 us
    all_to_all x1, blocking collectives, shards(): lax.all_to_all(partial, 'row', 0, 0, tiled=True, axis_index_groups=near_g...  20.8 us
    dot_general x9, matrix products, product(): lax.dot_general(left, right, (contract, ((), ())), precision=PRECISION, p...  17.1 us
    ppermute x6, starting transfers between devices, swapped(): return lax.ppermute(array, axis, [(i, i ^ 1) for i in range(size)])  16.3 us
    ppermute x4, starting transfers between devices, shifted(): lax.ppermute(array, axis, [(i, (i + step) % size) for i in range(size)])  13.7 us
    ppermute x6, waiting for transfers between devices, swapped(): return lax.ppermute(array, axis, [(i, i ^ 1) for i in range(size)])  11.6 us
  transfers between devices with their start and end apart: 12, of which 2 were waited for; matrix products, arithmetic and copies ran while one was open for 11% of the time, Pallas kernels for 0%

profile of v1, /device:TPU:41, one launch (start us, length us, event | category | flops | bytes accessed | tf_op | source)
XLA Modules:
  0.0 286.6 jit_solution(5933895443143171713)
XLA Ops:
  7.3 2.1 reshape.137
  9.4 3.5 %fusion.14 = (f32[256,2,256]{2,1,0:T(2,128)S(1)}, f32[256,2,256]{2,1,0:T(2,128)S(1)}) fusion(pred[]{:T(512)S(6)} %eq.14, f32[256,2,2,256]{3,2,1,0:T(2,128)S(1)} %reshape.137), kind=kLoop, calls=%fused_computation.19 | loop fusion | flops 262144 | bytes 2097153 | tf_op jit(solution)/shard_map/jit(_where)/select_n | solution.py:46
  13.0 4.4 %collective-permute-start.1 = (f32[256,512]{1,0:T(8,128)S(1)}, f32[256,512]{1,0:T(8,128)S(1)}, u32[]{:S(2)}, u32[]{:S(2)}) collective-permute-start(f32[256,512]{1,0:T(8,128)S(1)} %bitcast.36), channel_id=1, source_target_pairs={{0,8},{8,0},{16,24},{24,16},{32,40},{40,32},{48,56},{56,48},{64,72... | collective-permute-start | bytes 1572872 | tf_op jit(solution)/shard_map/ppermute | solution.py:17
  17.5 11.6 %collective-permute-done.1 = f32[256,512]{1,0:T(8,128)S(1)} collective-permute-done((f32[256,512]{1,0:T(8,128)S(1)}, f32[256,512]{1,0:T(8,128)S(1)}, u32[]{:S(2)}, u32[]{:S(2)}) %collective-permute-start.1) | collective-permute-done | bytes 524320 | tf_op jit(solution)/shard_map/ppermute | solution.py:17
  29.2 3.3 %collective-permute-start.3 = (f32[512,512]{1,0:T(8,128)S(1)}, f32[512,512]{1,0:T(8,128)S(1)}, u32[]{:S(2)}, u32[]{:S(2)}) collective-permute-start(f32[512,512]{1,0:T(8,128)S(1)} %constant_dynamic-update-slice_fusion), channel_id=1, source_target_pairs={{0,2},{2,4},{4,6},{6,0},{1,3},{3,5},{5,7},{7,1},{8,10},{10,12},{12... | collective-permute-start | bytes 3145736 | tf_op jit(solution)/shard_map/ppermute | solution.py:12
  32.5 3.5 %collective-permute-start.6 = (f32[512,512]{1,0:T(8,128)S(1)}, f32[512,512]{1,0:T(8,128)S(1)}, u32[]{:S(2)}, u32[]{:S(2)}) collective-permute-start(f32[512,512]{1,0:T(8,128)S(1)} %constant_dynamic-update-slice_fusion), channel_id=1, source_target_pairs={{0,6},{2,0},{4,2},{6,4},{1,7},{3,1},{5,3},{7,5},{8,14},{10,8},{12,... | collective-permute-start | bytes 3145736 | tf_op jit(solution)/shard_map/ppermute | solution.py:12
  36.0 3.1 %collective-permute-start = (f32[256,128]{1,0:T(8,128)S(1)}, f32[256,128]{1,0:T(8,128)S(1)}, u32[]{:S(2)}, u32[]{:S(2)}) collective-permute-start(f32[256,128]{1,0:T(8,128)S(1)} %copy-done.5), channel_id=1, source_target_pairs={{0,8},{8,0},{16,24},{24,16},{32,40},{40,32},{48,56},{56,48},{64,72... | collective-permute-start | bytes 393224 | tf_op jit(solution)/shard_map/ppermute | solution.py:17
  39.1 30.1 %all-gather = f32[1024,128]{1,0:T(8,128)} all-gather(f32[128,128]{1,0:T(8,128)S(1)} %get-tuple-element.11), channel_id=2, replica_groups=mesh['groups'=2,'row'=32,'col'=4,'sub'=2] {'col','sub'}, dimensions={0}, use_global_device_ids=true | all-gather | bytes 589824 | tf_op jit(solution)/shard_map/all_gather | solution.py:29
  70.1 3.5 %collective-permute-start.5 = (f32[256,512]{1,0:T(8,128)}, f32[256,512]{1,0:T(8,128)}, u32[]{:S(2)}, u32[]{:S(2)}) collective-permute-start(f32[256,512]{1,0:T(8,128)} %slice.38), channel_id=1, source_target_pairs={{0,2},{2,4},{4,6},{6,0},{1,3},{3,5},{5,7},{7,1},{8,10},{10,12},{12... | collective-permute-start | bytes 1572872 | tf_op jit(solution)/shard_map/ppermute | solution.py:12
  73.6 23.2 %all-gather.1 = f32[1024,128]{1,0:T(8,128)} all-gather(f32[128,128]{1,0:T(8,128)S(1)} %get-tuple-element.12), channel_id=3, replica_groups=mesh['groups'=2,'row'=32,'col'=4,'sub'=2] {'col','sub'}, dimensions={0}, use_global_device_ids=true | all-gather | bytes 589824 | tf_op jit(solution)/shard_map/all_gather | solution.py:29
  96.8 2.0 copy.19
  98.9 2.1 copy.20
  101.0 3.4 %collective-permute-start.7 = (f32[256,512]{1,0:T(8,128)S(1)}, f32[256,512]{1,0:T(8,128)S(1)}, u32[]{:S(2)}, u32[]{:S(2)}) collective-permute-start(f32[256,512]{1,0:T(8,128)S(1)} %slice.39), channel_id=1, source_target_pairs={{0,6},{2,0},{4,2},{6,4},{1,7},{3,1},{5,3},{7,5},{8,14},{10,8},{12,... | collective-permute-start | bytes 1572872 | tf_op jit(solution)/shard_map/ppermute | solution.py:12
  104.4 21.8 %all-gather.2 = f32[1024,128]{1,0:T(8,128)} all-gather(f32[128,128]{1,0:T(8,128)S(1)} %get-tuple-element.13), channel_id=4, replica_groups=mesh['groups'=2,'row'=32,'col'=4,'sub'=2] {'col','sub'}, dimensions={0}, use_global_device_ids=true | all-gather | bytes 589824 | tf_op jit(solution)/shard_map/all_gather | solution.py:29
  126.2 2.1 collective-permute-start.2
  128.3 1.9 constant_dynamic-update-slice_fusion.3
  131.0 2.3 collective-permute-start.8
  133.3 14.5 %all-gather.3 = f32[1024,128]{1,0:T(8,128)} all-gather(f32[128,128]{1,0:T(8,128)S(1)} %get-tuple-element.14), channel_id=5, replica_groups=mesh['groups'=2,'row'=32,'col'=4,'sub'=2] {'col','sub'}, dimensions={0}, use_global_device_ids=true | all-gather | bytes 589824 | tf_op jit(solution)/shard_map/all_gather | solution.py:29
  147.8 2.1 copy.21
  149.9 2.1 copy.22
  152.0 2.1 collective-permute-start.4
  154.1 2.3 collective-permute-start.9
  156.4 2.1 fusion.23
  158.5 2.3 fusion.20
  161.8 2.2 fusion.25
  164.0 2.2 fusion.18
  167.3 2.4 fusion.11
  169.7 2.2 fusion.8
  173.8 20.8 %all_to_all.15 = f32[4,8,32,128]{3,2,1,0:T(8,128)S(1)} all-to-all(f32[4,8,32,128]{3,2,1,0:T(8,128)S(1)} %bitcast.35), channel_id=1, replica_groups={{0,8,16,24},{32,40,48,56},{64,72,80,88},{96,104,112,120},{128,136,144,1..., dimensions={0} | all-to-all | bytes 1048576 | tf_op jit(solution)/shard_map/all_to_all | solution.py:73
  195.3 49.8 %all-to-all-start.1 = ((f32[8,32,128]{2,1,0:T(8,128)}), f32[8,32,128]{2,1,0:T(8,128)S(1)}, u32[]{:S(2)}, u32[]{:S(2)}) async-start(f32[8,32,128]{2,1,0:T(8,128)} %reduce_sum.18), calls=%async_computation.1 | async-start | bytes 262144 | tf_op jit(solution)/shard_map/all_to_all | solution.py:74
  245.8 23.3 %all-to-all-done.1 = f32[8,32,128]{2,1,0:T(8,128)S(1)} async-done(((f32[8,32,128]{2,1,0:T(8,128)}), f32[8,32,128]{2,1,0:T(8,128)S(1)}, u32[]{:S(2)}, u32[]{:S(2)}) %all-to-all-start.1) | async-done | bytes 131104 | tf_op jit(solution)/shard_map/all_to_all | solution.py:74
  269.1 9.9 %all_to_all.16 = f32[2,32,128]{2,1,0:T(8,128)S(1)} all-to-all(f32[2,32,128]{2,1,0:T(8,128)S(1)} %pad_maximum_fusion), channel_id=1, replica_groups=mesh['groups'=2,'row'=32,'col'=4,'sub'=2] {'sub'}, dimensions={0} | all-to-all | bytes 65536 | tf_op jit(solution)/shard_map/all_to_all | solution.py:78
  (45 shorter events, 8.0 us)
Async XLA Ops:
  6.5 149.8 %all-gather.6.cloned.1.call-start = ((), (), s32[]{:S(2)}) async-start(), calls=%async_computation.3 | async-start | bytes 2228224 | tf_op jit(solution)/shard_map/all_gather | solution.py:43
  13.0 23.0 %copy-start.5 = (f32[256,128]{1,0:T(8,128)S(1)}, f32[256,128]{1,0:T(8,128)}, u32[]{:S(2)}) copy-start(f32[256,128]{1,0:T(8,128)} %param.4) | copy-start | bytes 393220
  13.0 16.1 %collective-permute-start.1 = (f32[256,512]{1,0:T(8,128)S(1)}, f32[256,512]{1,0:T(8,128)S(1)}, u32[]{:S(2)}, u32[]{:S(2)}) collective-permute-start(f32[256,512]{1,0:T(8,128)S(1)} %bitcast.36), channel_id=1, source_target_pairs={{0,8},{8,0},{16,24},{24,16},{32,40},{40,32},{48,56},{56,48},{64,72... | collective-permute-start | bytes 1572872 | tf_op jit(solution)/shard_map/ppermute | solution.py:17
  29.2 40.1 %collective-permute-start.3 = (f32[512,512]{1,0:T(8,128)S(1)}, f32[512,512]{1,0:T(8,128)S(1)}, u32[]{:S(2)}, u32[]{:S(2)}) collective-permute-start(f32[512,512]{1,0:T(8,128)S(1)} %constant_dynamic-update-slice_fusion), channel_id=1, source_target_pairs={{0,2},{2,4},{4,6},{6,0},{1,3},{3,5},{5,7},{7,1},{8,10},{10,12},{12... | collective-permute-start | bytes 3145736 | tf_op jit(solution)/shard_map/ppermute | solution.py:12
  32.5 68.5 %collective-permute-start.6 = (f32[512,512]{1,0:T(8,128)S(1)}, f32[512,512]{1,0:T(8,128)S(1)}, u32[]{:S(2)}, u32[]{:S(2)}) collective-permute-start(f32[512,512]{1,0:T(8,128)S(1)} %constant_dynamic-update-slice_fusion), channel_id=1, source_target_pairs={{0,6},{2,0},{4,2},{6,4},{1,7},{3,1},{5,3},{7,5},{8,14},{10,8},{12,... | collective-permute-start | bytes 3145736 | tf_op jit(solution)/shard_map/ppermute | solution.py:12
  36.0 68.4 %collective-permute-start = (f32[256,128]{1,0:T(8,128)S(1)}, f32[256,128]{1,0:T(8,128)S(1)}, u32[]{:S(2)}, u32[]{:S(2)}) collective-permute-start(f32[256,128]{1,0:T(8,128)S(1)} %copy-done.5), channel_id=1, source_target_pairs={{0,8},{8,0},{16,24},{24,16},{32,40},{40,32},{48,56},{56,48},{64,72... | collective-permute-start | bytes 393224 | tf_op jit(solution)/shard_map/ppermute | solution.py:17
  70.1 58.2 %collective-permute-start.5 = (f32[256,512]{1,0:T(8,128)}, f32[256,512]{1,0:T(8,128)}, u32[]{:S(2)}, u32[]{:S(2)}) collective-permute-start(f32[256,512]{1,0:T(8,128)} %slice.38), channel_id=1, source_target_pairs={{0,2},{2,4},{4,6},{6,0},{1,3},{3,5},{5,7},{7,1},{8,10},{10,12},{12... | collective-permute-start | bytes 1572872 | tf_op jit(solution)/shard_map/ppermute | solution.py:12
  101.0 29.2 %collective-permute-start.7 = (f32[256,512]{1,0:T(8,128)S(1)}, f32[256,512]{1,0:T(8,128)S(1)}, u32[]{:S(2)}, u32[]{:S(2)}) collective-permute-start(f32[256,512]{1,0:T(8,128)S(1)} %slice.39), channel_id=1, source_target_pairs={{0,6},{2,0},{4,2},{6,4},{1,7},{3,1},{5,3},{7,5},{8,14},{10,8},{12,... | collective-permute-start | bytes 1572872 | tf_op jit(solution)/shard_map/ppermute | solution.py:12
  126.2 35.6 %collective-permute-start.2 = (f32[512,512]{1,0:T(8,128)S(1)}, f32[512,512]{1,0:T(8,128)}, u32[]{:S(2)}, u32[]{:S(2)}) collective-permute-start(f32[512,512]{1,0:T(8,128)S(1)} %constant_dynamic-update-slice_fusion), channel_id=1, source_target_pairs={{0,1},{1,0},{2,3},{3,2},{4,5},{5,4},{6,7},{7,6},{8,9},{9,8},{10,11... | collective-permute-start | bytes 3145736 | tf_op jit(solution)/shard_map/ppermute | solution.py:17
  131.0 33.0 %collective-permute-start.8 = (f32[512,512]{1,0:T(8,128)}, f32[512,512]{1,0:T(8,128)}, u32[]{:S(2)}, u32[]{:S(2)}) collective-permute-start(f32[512,512]{1,0:T(8,128)} %constant_dynamic-update-slice_fusion.2), channel_id=1, source_target_pairs={{0,1},{1,0},{2,3},{3,2},{4,5},{5,4},{6,7},{7,6},{8,9},{9,8},{10,11... | collective-permute-start | bytes 3145736 | tf_op jit(solution)/shard_map/ppermute | solution.py:17
  152.0 15.3 %collective-permute-start.4 = (f32[512,512]{1,0:T(8,128)S(1)}, f32[512,512]{1,0:T(8,128)}, u32[]{:S(2)}, u32[]{:S(2)}) collective-permute-start(f32[512,512]{1,0:T(8,128)S(1)} %collective-permute-done.3), channel_id=1, source_target_pairs={{0,1},{1,0},{2,3},{3,2},{4,5},{5,4},{6,7},{7,6},{8,9},{9,8},{10,11... | collective-permute-start | bytes 3145736 | tf_op jit(solution)/shard_map/ppermute | solution.py:17
  154.1 15.6 %collective-permute-start.9 = (f32[512,512]{1,0:T(8,128)S(1)}, f32[512,512]{1,0:T(8,128)}, u32[]{:S(2)}, u32[]{:S(2)}) collective-permute-start(f32[512,512]{1,0:T(8,128)S(1)} %collective-permute-done.6), channel_id=1, source_target_pairs={{0,1},{1,0},{2,3},{3,2},{4,5},{5,4},{6,7},{7,6},{8,9},{9,8},{10,11... | collective-permute-start | bytes 3145736 | tf_op jit(solution)/shard_map/ppermute | solution.py:17
  156.4 4.4 %copy-start = (f32[4096,128]{1,0:T(8,128)S(1)}, f32[4096,128]{1,0:T(8,128)}, u32[]{:S(2)}) copy-start(f32[4096,128]{1,0:T(8,128)} %all-gather.6.cloned.1.call-done) | copy-start | bytes 6291460
  167.2 4.7 %copy-start.1 = (f32[8,128,128]{1,2,0:T(8,128)S(1)}, f32[8,128,128]{1,2,0:T(8,128)}, u32[]{:S(2)}) copy-start(f32[8,128,128]{1,2,0:T(8,128)} %copy.19) | copy-start | bytes 1572868
  167.2 4.7 %copy-start.2 = (f32[8,128,128]{1,2,0:T(8,128)S(1)}, f32[8,128,128]{1,2,0:T(8,128)}, u32[]{:S(2)}) copy-start(f32[8,128,128]{1,2,0:T(8,128)} %copy.20) | copy-start | bytes 1572868
  167.3 4.7 %copy-start.3 = (f32[8,128,128]{1,2,0:T(8,128)S(1)}, f32[8,128,128]{1,2,0:T(8,128)}, u32[]{:S(2)}) copy-start(f32[8,128,128]{1,2,0:T(8,128)} %copy.21) | copy-start | bytes 1572868
  167.3 4.7 %copy-start.4 = (f32[8,128,128]{1,2,0:T(8,128)S(1)}, f32[8,128,128]{1,2,0:T(8,128)}, u32[]{:S(2)}) copy-start(f32[8,128,128]{1,2,0:T(8,128)} %copy.22) | copy-start | bytes 1572868
  195.3 73.8 %all-to-all-start.1 = ((f32[8,32,128]{2,1,0:T(8,128)}), f32[8,32,128]{2,1,0:T(8,128)S(1)}, u32[]{:S(2)}, u32[]{:S(2)}) async-start(f32[8,32,128]{2,1,0:T(8,128)} %reduce_sum.18), calls=%async_computation.1 | async-start | bytes 262144 | tf_op jit(solution)/shard_map/all_to_all | solution.py:74
Sparse Core Ops, SparseCore 0:
  9.4 122.9 all-gather.5
